TPU v7x, 8 devices: a whole 2x2x1 slice. The times are simulated.
8 devices in a mesh: dp: 1 (over z), cols: 2 (over y), rows: 4 (over x, core).
Axes of the slice: x: 2, y: 2, z: 1, core: 2. Of those that a mesh axis runs over, the one named last changes fastest.
Arguments:
- frames: bfloat16 [32, 2, 128, 96, 4], P(None, 'dp', 'rows', 'cols')
- w_in: bfloat16 [3, 3, 4, 256], replicated
- w_rec: bfloat16 [3, 3, 64, 256], replicated
- gate_bias: float32 [256], replicated
- h_init: bfloat16 [2, 128, 96, 64], P('dp', 'rows', 'cols')
- c_init: float32 [2, 128, 96, 64], P('dp', 'rows', 'cols')
Outputs:
- output 1: bfloat16 [32, 2, 128, 96, 64], P(None, 'dp', 'rows', 'cols')
- output 2: float32 [2, 128, 96, 64], P('dp', 'rows', 'cols')
All inputs are finite; a program needn't handle non-finite values.
Results may differ from a plain program's by a relative error of at most 0.00440778.
Values are sent between devices in bfloat16 or wider.
A program may use at most 1 GiB of HBM per device.

v0:
```python
import jax
import jax.numpy as jnp
from jax import lax
from jax.sharding import PartitionSpec as P, NamedSharding

CONV_DIMS = ("NHWC", "HWIO", "NHWC")


def conv_valid(operand, kernel):
    return lax.conv_general_dilated(operand, kernel, (1, 1), "VALID", dimension_numbers=CONV_DIMS, preferred_element_type=jnp.float32)


def cell_update(gate_pre, c_prev):
    gate_i, gate_f, gate_o, gate_g = jnp.split(gate_pre, 4, axis=-1)
    c_next = jax.nn.sigmoid(gate_f) * c_prev + jax.nn.sigmoid(gate_i) * jnp.tanh(gate_g)
    h_next = (jax.nn.sigmoid(gate_o) * jnp.tanh(c_next)).astype(jnp.bfloat16)
    return h_next, c_next


def edge_exchange(tile_in, axis_name, axis_size, axis_dim, width):
    length = tile_in.shape[axis_dim]
    low_part = lax.slice_in_dim(tile_in, 0, width, axis=axis_dim)
    high_part = lax.slice_in_dim(tile_in, length - width, length, axis=axis_dim)
    if axis_size == 1:
        from_prev = jnp.zeros_like(high_part)
        from_next = jnp.zeros_like(low_part)
    else:
        forward = [(source, source + 1) for source in range(axis_size - 1)]
        backward = [(source + 1, source) for source in range(axis_size - 1)]
        from_prev = lax.ppermute(high_part, axis_name, forward)
        from_next = lax.ppermute(low_part, axis_name, backward)
    return jnp.concatenate([from_prev, tile_in, from_next], axis=axis_dim)


def add_halo(tile_in, width, n_rows, n_cols):
    row_dim = tile_in.ndim - 3
    tall_tile = edge_exchange(tile_in, "rows", n_rows, row_dim, width)
    return edge_exchange(tall_tile, "cols", n_cols, row_dim + 1, width)


def solution(mesh):
    n_rows = mesh.shape["rows"]
    n_cols = mesh.shape["cols"]
    seq_spec = P(None, "dp", "rows", "cols", None)
    state_spec = P("dp", "rows", "cols", None)

    def local_run(frames, w_in, w_rec, gate_bias, h_init, c_init):
        frames_ext = add_halo(frames, 1, n_rows, n_cols)

        def time_step(carry_in, frame_ext):
            h_prev, c_prev = carry_in
            h_ext = add_halo(h_prev, 1, n_rows, n_cols)
            gate_pre = conv_valid(frame_ext, w_in) + conv_valid(h_ext, w_rec) + gate_bias
            h_next, c_next = cell_update(gate_pre, c_prev)
            return (h_next, c_next), h_next

        (h_last, c_last), hidden_seq = lax.scan(time_step, (h_init, c_init), frames_ext)
        return hidden_seq, c_last

    return jax.shard_map(local_run, mesh=mesh, in_specs=(seq_spec, P(), P(), P(), state_spec, state_spec), out_specs=(seq_spec, state_spec), check_vma=False)
```

profile of v0, /device:TPU:1, one launch (start us, length us, event | category | flops | bytes accessed | tf_op | source)
XLA Modules:
  0.0 917.2 jit_solution(3398047078673023065)
XLA Ops:
  1.6 4.5 collective-permute-start.4
  8.0 5.7 copy.34
  13.8 5.1 copy.33
  18.9 4.6 copy.35
  32.9 9.4 %pad_maximum_fusion.3 = bf16[32,2,34,50,4]{2,4,3,1,0:T(4,128)(2,1)} fusion(bf16[32,2,34,1,4]{2,4,3,1,0:T(4,128)(2,1)S(1)} %collective-permute-done.7, bf16[32,2,1,48,4]{2,4,3,1,0:T(4,128)(2,1)} %copy.35, bf16[32,2,32,48,4]{2,4,3,1,0:T(4,128)(2,1)S(1)} %copy-done.1, bf16[32,2,1,48,4]{2,4,3,1,0:T(4,128)(2,1)} %copy.33, ...), kind=kLoop, calls=%fused_computation.35 | loop fusion | flops 4352000 | bytes 1740800 | tf_op jit(solution)/shard_map/concatenate | solution.py:32
  42.3 872.8 %while.14 = (s32[]{:T(128)}, bf16[2,32,48,64]{3,1,2,0:T(8,128)(2,1)S(1)}, f32[2,32,48,64]{3,1,2,0:T(8,128)S(1)}, bf16[32,2,32,48,64]{4,3,2,1,0:T(8,128)(2,1)}, b...) while((s32[]{:T(128)}, ...), condition=%wide.region_1.2_spmd, body=%wide.region_0.1_spmd.sunk | while | flops 1134000896 | bytes 49181612 | solution.py:57
  44.5 5.1 collective-permute-start.1
  72.4 4.5 collective-permute-start.1
  99.6 4.5 collective-permute-start.1
  126.9 4.5 collective-permute-start.1
  154.1 4.5 collective-permute-start.1
  181.4 4.5 collective-permute-start.1
  208.6 4.5 collective-permute-start.1
  235.9 4.5 collective-permute-start.1
  263.1 4.5 collective-permute-start.1
  290.4 4.5 collective-permute-start.1
  317.6 4.5 collective-permute-start.1
  344.9 4.5 collective-permute-start.1
  372.1 4.5 collective-permute-start.1
  399.4 4.5 collective-permute-start.1
  426.6 4.5 collective-permute-start.1
  453.9 4.5 collective-permute-start.1
  508.4 4.5 collective-permute-start.1
  535.6 4.5 collective-permute-start.1
  590.1 4.5 collective-permute-start.1
  617.4 4.5 collective-permute-start.1
  671.9 4.5 collective-permute-start.1
  699.1 4.5 collective-permute-start.1
  753.6 4.5 collective-permute-start.1
  780.9 4.5 collective-permute-start.1
  835.4 4.5 collective-permute-start.1
  862.6 4.5 collective-permute-start.1
  (961 shorter events, 764.4 us)
Async XLA Ops:
  1.6 12.2 %collective-permute-start.4 = (bf16[32,2,1,48,4]{3,0,4,2,1:T(8,128)(2,1)S(1)}, bf16[32,2,1,48,4]{3,0,4,2,1:T(8,128)(2,1)S(1)}, u32[]{:S(2)}, u32[]{:S(2)}) collective-permute-start(bf16[32,2,1,48,4]{3,0,4,2,1:T(8,128)(2,1)S(1)} %copy.45), channel_id=1, source_target_pairs={{0,1},{1,2},{2,3},{4,5},{5,6},{6,7}} | collective-permute-start | bytes 73736 | tf_op jit(solution)/shard_map/ppermute | solution.py:30
  6.1 12.8 %collective-permute-start.5 = (bf16[32,2,1,48,4]{3,0,4,2,1:T(8,128)(2,1)S(1)}, bf16[32,2,1,48,4]{3,0,4,2,1:T(8,128)(2,1)S(1)}, u32[]{:S(2)}, u32[]{:S(2)}) collective-permute-start(bf16[32,2,1,48,4]{3,0,4,2,1:T(8,128)(2,1)S(1)} %copy.46), channel_id=1, source_target_pairs={{1,0},{2,1},{3,2},{5,4},{6,5},{7,6}} | collective-permute-start | bytes 73736 | tf_op jit(solution)/shard_map/ppermute | solution.py:31
  42.6 8.5 collective-permute-start
  51.1 8.2 collective-permute-start.2
  78.4 8.2 collective-permute-start.2
  105.6 8.2 collective-permute-start.2
  132.9 8.2 collective-permute-start.2
  160.1 8.2 collective-permute-start.2
  187.4 8.2 collective-permute-start.2
  214.6 8.2 collective-permute-start.2
  241.9 8.2 collective-permute-start.2
  269.1 8.2 collective-permute-start.2
  296.4 8.2 collective-permute-start.2
  323.6 8.2 collective-permute-start.2
  350.9 8.2 collective-permute-start.2
  378.1 8.2 collective-permute-start.2
  405.4 8.2 collective-permute-start.2
  432.6 8.2 collective-permute-start.2
  459.9 8.2 collective-permute-start.2
  487.1 8.2 collective-permute-start.2
  514.4 8.2 collective-permute-start.2
  541.6 8.2 collective-permute-start.2
  568.9 8.2 collective-permute-start.2
  596.1 8.2 collective-permute-start.2
  623.4 8.2 collective-permute-start.2
  650.6 8.2 collective-permute-start.2
  677.9 8.2 collective-permute-start.2
  705.1 8.2 collective-permute-start.2
  759.6 8.2 collective-permute-start.2
  786.9 8.2 collective-permute-start.2
  841.4 8.2 collective-permute-start.2
  868.6 8.2 collective-permute-start.2
  (138 other events, 827.3 us)
where the time goes:
time: 921 us; the launch traced here: 917 us
  starting transfers between devices  385 us (42%)
  local copies, waits for them, and re-layouts  220 us (24%)
  other arithmetic  157 us (17%)
  matrix products  148 us (16%)
    ppermute x66, starting transfers between devices, edge_exchange(): from_prev = lax.ppermute(high_part, axis_name, forward)  279 us
    conv_general_dilated x64, matrix products, conv_valid(): lax.conv_general_dilated(operand, kernel, (1, 1), 'VALID', dimension_numb...  148 us
    ppermute x66, starting transfers between devices, edge_exchange(): from_next = lax.ppermute(low_part, axis_name, backward)  106 us
    div x32, other arithmetic, cell_update(): jax.nn.sigmoid(gate_f) * c_prev + jax.nn.sigmoid(gate_i) * jnp.tanh(gate_g)  54.2 us
    conv_general_dilated x64, other arithmetic, conv_valid(): lax.conv_general_dilated(operand, kernel, (1, 1), 'VALID', dimension_numb...  46.2 us
    dynamic_update_slice x32, local copies, waits for them, and re-layouts, local_run(): lax.scan(time_step, (h_init, c_init), frames_ext)  38.1 us
    div x64, local copies, waits for them, and re-layouts, cell_update(): jax.nn.sigmoid(gate_f) * c_prev + jax.nn.sigmoid(gate_i) * jnp.tanh(gate_g)  37.9 us
    squeeze x64, local copies, waits for them, and re-layouts, local_run(): lax.scan(time_step, (h_init, c_init), frames_ext)  31.9 us
  transfers between devices with their start and end apart: 132, of which 1 were waited for; matrix products, arithmetic and copies ran while one was open for 17% of the time, Pallas kernels for 0%

commit v1 on v0

v1 whole, which is shorter than its diff:
```python
import jax
import jax.numpy as jnp
from jax import lax
from jax.experimental import pallas as pl
from jax.experimental.pallas import tpu as pltpu
from jax.sharding import PartitionSpec as P

MESH = pl.DeviceIdType.MESH
F32, BF16 = jnp.float32, jnp.bfloat16

STEPS = 32
SAMPLES = 2
TILE_H = 32
TILE_W = 48
C_IN = 4
C_HID = 64
ROUND = 4
ROUNDS = STEPS // ROUND
EXT = 8
PITCH = TILE_W + EXT
ROW = SAMPLES * PITCH
ROWS = TILE_H + 2 * ROUND
CELLS = ROWS * ROW
PAD = 8
LANES = 128
EDGE = ROUND * SAMPLES * TILE_W
HALF = LANES // 2


def chunk_rows(count):
    for rows in (9, 8, 19, 17):
        if count % rows == 0:
            return rows
    raise ValueError(count)


def kernel(frames_ref, state_ref, w_ref, bias_ref, seq_ref, c_out_ref,
           h_buf, c_buf, g_buf, a_buf, out_buf, gain_buf,
           up_buf, down_buf, edge_buf, from_up, from_down, from_edge,
           send_sem, recv_sem, out_sem):
    row = lax.axis_index("rows")
    col = lax.axis_index("cols")
    has_up = row > 0
    has_down = row < lax.axis_size("rows") - 1
    is_left = col == 0
    other = 1 - col

    own_at = jnp.where(is_left, 0, EXT)
    edge_at = jnp.where(is_left, TILE_W - EXT, EXT)
    halo_at = jnp.where(is_left, TILE_W, 0)

    lane = lax.broadcasted_iota(jnp.int32, (EXT, LANES), 1)
    cell = lax.broadcasted_iota(jnp.int32, (EXT, LANES), 0)
    low = lane < HALF
    halo_cell = jnp.where(is_left, (cell < ROUND).astype(F32), (cell >= EXT - ROUND).astype(F32))

    def low_mask(cells):
        return lax.broadcasted_iota(jnp.int32, (cells, LANES), 1) < HALF

    zero_h = jnp.zeros((ROW, LANES), F32)
    zero_a = jnp.zeros((ROW, 2 * LANES), BF16)
    pad = jnp.zeros((PAD, LANES), F32)
    for buf in (h_buf, c_buf, g_buf):
        buf[pl.ds(0, PAD), :] = pad
        buf[pl.ds(PAD + CELLS, PAD), :] = pad

    @pl.loop(0, ROWS)
    def _(y):
        at = pl.multiple_of(y * ROW, ROW)
        h_buf[pl.ds(PAD + at, ROW), :] = zero_h
        c_buf[pl.ds(PAD + at, ROW), :] = zero_h
        g_buf[pl.ds(PAD + at, ROW), :] = zero_h
        a_buf[pl.ds(at, ROW), :] = zero_a
        for slot in range(3):
            from_edge[slot, pl.ds(pl.multiple_of(y * EXT, EXT), EXT), :] = pad

    gain = jnp.where(low, 0.5, 1.0)
    shift = jnp.where(low, 0.5, 0.0)
    for s in range(SAMPLES):
        for v in range(PITCH // EXT):
            at = s * PITCH + v * EXT
            is_halo = halo_at == v * EXT
            keep = jnp.where(is_halo, halo_cell, 1.0)
            gain_buf[0, pl.ds(at, EXT), :] = gain * keep
            gain_buf[1, pl.ds(at, EXT), :] = shift * keep

    barrier = pltpu.get_barrier_semaphore()

    def greet(target):
        pl.semaphore_signal(barrier, inc=1, device_id=target, device_id_type=MESH)

    greet({"cols": other})

    @pl.when(has_up)
    def _():
        greet({"rows": row - 1})
        greet({"rows": row - 1, "cols": other})

    @pl.when(has_down)
    def _():
        greet({"rows": row + 1})
        greet({"rows": row + 1, "cols": other})

    pl.semaphore_wait(barrier, 1 + 2 * has_up.astype(jnp.int32) + 2 * has_down.astype(jnp.int32))

    def copies(slot):
        def copy(src, dst, index, target):
            return pltpu.make_async_remote_copy(
                src_ref=src, dst_ref=dst, send_sem=send_sem.at[slot, index],
                recv_sem=recv_sem.at[slot, index], device_id=target, device_id_type=MESH)

        edge = edge_buf.at[slot]
        halo = from_edge.at[slot]
        corner = ROUND * EXT
        own = TILE_H * EXT
        return (
            copy(up_buf.at[slot], from_down.at[slot], 0, {"rows": row - 1}),
            copy(down_buf.at[slot], from_up.at[slot], 1, {"rows": row + 1}),
            copy(edge, halo.at[pl.ds(corner, own)], 2, {"cols": other}),
            copy(edge.at[pl.ds(0, corner)], halo.at[pl.ds(corner + own, corner)], 3, {"rows": row - 1, "cols": other}),
            copy(edge.at[pl.ds(own - corner, corner)], halo.at[pl.ds(0, corner)], 4, {"rows": row + 1, "cols": other}),
        )

    def send(slot, read):
        for r in range(ROUND):
            for s in range(SAMPLES):
                to = pl.ds((r * SAMPLES + s) * TILE_W, TILE_W)
                at = pl.multiple_of((ROUND + r) * ROW + s * PITCH + own_at, EXT)
                up_buf[slot, to, :] = read(at, TILE_W)
                at = pl.multiple_of((TILE_H + r) * ROW + s * PITCH + own_at, EXT)
                down_buf[slot, to, :] = read(at, TILE_W)

        @pl.loop(0, TILE_H)
        def _(y):
            first = read(pl.multiple_of((ROUND + y) * ROW + edge_at, EXT), EXT)
            second = read(pl.multiple_of((ROUND + y) * ROW + PITCH + edge_at, EXT), EXT)
            first = jnp.where(is_left, pltpu.roll(first, EXT // 2, 0), first)
            second = jnp.where(is_left, second, pltpu.roll(second, EXT // 2, 0))
            edge_buf[slot, pl.ds(pl.multiple_of(y * EXT, EXT), EXT), :] = jnp.where(cell < EXT // 2, first, second)

        up, down, across, across_up, across_down = copies(slot)
        across.start()

        @pl.when(has_up)
        def _():
            up.start()
            across_up.start()

        @pl.when(has_down)
        def _():
            down.start()
            across_down.start()

    def receive(slot, write):
        up, down, across, across_up, across_down = copies(slot)
        across.wait_send()
        across.wait_recv()

        @pl.when(has_up)
        def _():
            up.wait_send()
            across_up.wait_send()
            down.wait_recv()
            across_down.wait_recv()
            for r in range(ROUND):
                for s in range(SAMPLES):
                    frm = pl.ds((r * SAMPLES + s) * TILE_W, TILE_W)
                    write(pl.multiple_of(r * ROW + s * PITCH + own_at, EXT), from_up[slot, frm, :])

        @pl.when(has_down)
        def _():
            down.wait_send()
            across_down.wait_send()
            up.wait_recv()
            across_up.wait_recv()
            for r in range(ROUND):
                for s in range(SAMPLES):
                    frm = pl.ds((r * SAMPLES + s) * TILE_W, TILE_W)
                    write(pl.multiple_of((ROUND + TILE_H + r) * ROW + s * PITCH + own_at, EXT), from_down[slot, frm, :])

        @pl.loop(0, ROWS)
        def _(y):
            got = from_edge[slot, pl.ds(pl.multiple_of(y * EXT, EXT), EXT), :]
            turned = pltpu.roll(got, EXT // 2, 0)
            write(pl.multiple_of(y * ROW + halo_at, EXT), jnp.where(is_left, got, turned) * halo_cell)
            write(pl.multiple_of(y * ROW + PITCH + halo_at, EXT), jnp.where(is_left, turned, got) * halo_cell)

    def read_frames(at, cells):
        return g_buf[pl.ds(PAD + at, cells), :]

    def write_frames(at, value):
        g_buf[pl.ds(PAD + at, value.shape[0]), :] = value

    def read_state(at, cells):
        return jnp.where(low_mask(cells), h_buf[pl.ds(PAD + at, cells), :], c_buf[pl.ds(PAD + at, cells), :])

    def write_state(at, value):
        cells = value.shape[0]
        h_buf[pl.ds(PAD + at, cells), :] = value
        c_buf[pl.ds(PAD + at, cells), :] = jnp.where(low_mask(cells), pltpu.roll(value, HALF, 1), value)

    @pl.loop(0, TILE_H)
    def _(y):
        for s in range(SAMPLES):
            at = pl.multiple_of((ROUND + y) * ROW + s * PITCH + own_at, EXT)
            write_frames(at, frames_ref[y, s, :, :].astype(F32))
            write_state(at, state_ref[y, s, :, :])

    send(2, read_frames)
    send(0, read_state)
    receive(2, write_frames)

    def build(y, with_frames, turn):
        at = pl.multiple_of(y * ROW, ROW)
        mine = h_buf[pl.ds(PAD + at, ROW), :]
        before = h_buf[pl.ds(PAD - 1 + at, ROW), :]
        after = h_buf[pl.ds(PAD + 1 + at, ROW), :]
        low_row = low_mask(ROW)
        a_buf[pl.ds(at, ROW), 0:LANES] = jnp.where(low_row, mine, pltpu.roll(before, HALF, 1)).astype(BF16)
        if with_frames:
            lane_row = lax.broadcasted_iota(jnp.int32, (ROW, LANES), 1)
            f_mine = pltpu.roll(g_buf[pl.ds(PAD + at, ROW), :], turn(80), 1)
            f_before = pltpu.roll(g_buf[pl.ds(PAD - 1 + at, ROW), :], turn(64), 1)
            f_after = pltpu.roll(g_buf[pl.ds(PAD + 1 + at, ROW), :], turn(96), 1)
            f = jnp.where(lane_row < 80, f_before, jnp.where(lane_row < 96, f_mine, f_after))
            a_buf[pl.ds(at, ROW), LANES:2 * LANES] = jnp.where(low_row, after, f).astype(BF16)
        else:
            a_buf[pl.ds(at, ROW), LANES:LANES + HALF] = after[:, 0:HALF].astype(BF16)

    def advance(y, rows, step, slot):
        at = pl.multiple_of(y * ROW, ROW)
        gates = jnp.zeros((rows * ROW, 2 * LANES), F32)
        for dy in range(3):
            left = a_buf[pl.ds(pl.multiple_of(at + (dy - 1) * ROW, ROW), rows * ROW), :]
            gates = gates + jnp.dot(left, w_ref[step, dy, :, :], preferred_element_type=F32)
        low_row = low_mask(ROW)
        for r in range(rows):
            part = slice(r * ROW, (r + 1) * ROW)
            here = pl.ds(PAD + at + r * ROW, ROW)
            first = jnp.tanh(gates[part, 0:LANES] + bias_ref[0:1, :])
            second = jnp.tanh(gates[part, LANES:] + bias_ref[1:2, :])
            mixed = (0.5 * first + 0.5) * jnp.where(low_row, c_buf[here, :], second)
            c_next = mixed + pltpu.roll(mixed, HALF, 1)
            c_buf[here, :] = c_next
            h_next = (second * gain_buf[0, :, :] + gain_buf[1, :, :]) * jnp.tanh(c_next)
            h_buf[here, :] = h_next
            for s in range(SAMPLES):
                own = jnp.where(is_left, h_next[s * PITCH:s * PITCH + TILE_W, :], h_next[s * PITCH + EXT:(s + 1) * PITCH, :])
                out_buf[slot, s, y + r, :, :] = own[:, 0:C_HID].astype(BF16)

    def out_copy(t, slot):
        return pltpu.make_async_copy(
            out_buf.at[slot, :, pl.ds(ROUND, TILE_H)], seq_ref.at[t], out_sem.at[slot])

    @pl.loop(0, ROUNDS)
    def _(n):
        receive(n % 2, write_state)

        def turn(lane_to):
            return lax.rem(lane_to + LANES - ROUND * C_IN * n, LANES)

        for j in range(1, ROUND + 1):
            step = j - 1
            t = ROUND * n + step
            slot = step % 2

            @pl.when(t >= 2)
            def _():
                out_copy(t - 2, slot).wait()

            def build_own(y):
                build(y, j == 1, turn)

            for y in range(j - 1, ROUND):
                pl.when(has_up)(lambda y=y: build_own(y))
            for y in range(ROUND + TILE_H, ROWS - j + 1):
                pl.when(has_down)(lambda y=y: build_own(y))
            pl.loop(ROUND, ROUND + TILE_H)(build_own)

            count = ROWS - 2 * j
            rows = chunk_rows(count)
            pl.loop(0, count // rows)(lambda i: advance(j + i * rows, rows, step, slot))
            out_copy(t, slot).start()

        @pl.when(n < ROUNDS - 1)
        def _():
            send((n + 1) % 2, read_state)

    for t in (STEPS - 2, STEPS - 1):
        out_copy(t, t % 2).wait()

    @pl.loop(0, TILE_H)
    def _(y):
        for s in range(SAMPLES):
            at = pl.multiple_of((ROUND + y) * ROW + s * PITCH + own_at, EXT)
            c_out_ref[s, y, :, :] = c_buf[pl.ds(PAD + at, TILE_W), 0:C_HID]


def pack_weights(w_in, w_rec):
    def gates(w):
        i, f, o, g = jnp.split(w, 4, axis=-1)
        half = jnp.asarray(0.5, w.dtype)
        return jnp.concatenate([f * half, i * half, o * half, g], axis=-1)

    rec = gates(w_rec)
    rec = jnp.concatenate([rec[:, 1], rec[:, 0], rec[:, 2]], axis=1)
    inp = gates(w_in)
    rest = LANES - HALF - 3 * ROUND * C_IN
    packed = []
    for step in range(ROUND):
        spread = jnp.pad(inp, ((0, 0), (0, 0), (step * C_IN, (ROUND - 1 - step) * C_IN), (0, 0)))
        spread = spread.reshape(3, 3 * ROUND * C_IN, 4 * C_HID)
        packed.append(jnp.concatenate([rec, jnp.pad(spread, ((0, 0), (0, rest), (0, 0)))], axis=1))
    return jnp.stack(packed)


def pack_bias(bias):
    i, f, o, g = jnp.split(bias, 4)
    return jnp.stack([jnp.concatenate([f, i]) * 0.5, jnp.concatenate([o * 0.5, g])])


def solution(mesh):
    assert mesh.shape["cols"] == 2
    seq_spec = P(None, "dp", "rows", "cols", None)
    state_spec = P("dp", "rows", "cols", None)

    def local_run(frames, w_in, w_rec, gate_bias, h_init, c_init):
        frames_cells = frames.transpose(2, 1, 3, 0, 4).reshape(TILE_H, SAMPLES, TILE_W, STEPS * C_IN)
        state = jnp.concatenate([h_init.astype(F32), c_init], axis=-1).transpose(1, 0, 2, 3)
        vmem = pl.BlockSpec(memory_space=pltpu.VMEM)
        return pl.pallas_call(
            kernel,
            out_shape=(
                jax.ShapeDtypeStruct((STEPS, SAMPLES, TILE_H, TILE_W, C_HID), BF16),
                jax.ShapeDtypeStruct((SAMPLES, TILE_H, TILE_W, C_HID), F32),
            ),
            in_specs=[vmem] * 4,
            out_specs=(pl.BlockSpec(memory_space=pl.ANY), vmem),
            scratch_shapes=[
                pltpu.VMEM((CELLS + 2 * PAD, LANES), F32),
                pltpu.VMEM((CELLS + 2 * PAD, LANES), F32),
                pltpu.VMEM((CELLS + 2 * PAD, LANES), F32),
                pltpu.VMEM((CELLS, 2 * LANES), BF16),
                pltpu.VMEM((2, SAMPLES, ROWS, TILE_W, C_HID), BF16),
                pltpu.VMEM((2, ROW, LANES), F32),
                pltpu.VMEM((3, EDGE, LANES), F32),
                pltpu.VMEM((3, EDGE, LANES), F32),
                pltpu.VMEM((3, TILE_H * EXT, LANES), F32),
                pltpu.VMEM((3, EDGE, LANES), F32),
                pltpu.VMEM((3, EDGE, LANES), F32),
                pltpu.VMEM((3, ROWS * EXT, LANES), F32),
                pltpu.SemaphoreType.DMA((3, 5)),
                pltpu.SemaphoreType.DMA((3, 5)),
                pltpu.SemaphoreType.DMA((2,)),
            ],
            compiler_params=pltpu.CompilerParams(
                collective_id=0, has_side_effects=True, vmem_limit_bytes=48 * 1024 * 1024),
            name="convlstm",
        )(frames_cells, state, pack_weights(w_in, w_rec), pack_bias(gate_bias))

    return jax.shard_map(
        local_run, mesh=mesh, in_specs=(seq_spec, P(), P(), P(), state_spec, state_spec),
        out_specs=(seq_spec, state_spec), check_vma=False)
```

time: 921 us -> 295 us (0.32)
  starting transfers between devices: 385 us -> 0 us
  Pallas kernels: 0 us -> 255 us
  local copies, waits for them, and re-layouts: 220 us -> 34.6 us
  other arithmetic: 157 us -> 3.25 us
  matrix products: 148 us -> 0 us
    ppermute x132 -> x0, starting transfers between devices: 385 us -> none  [the longest x66 279 us: edge_exchange(): from_prev = lax.ppermute(high_part, axis_name, forward)]
    pallas_call x0 -> x1, Pallas kernels: none -> 255 us  [local_run(): pl.pallas_call(kernel, out_shape=(jax.ShapeDtypeStruct((STEPS, SAMPLES, T...]
    conv_general_dilated x64 -> x0, matrix products: 148 us -> none  [conv_valid(): lax.conv_general_dilated(operand, kernel, (1, 1), 'VALID', dimension_numb...]
    div x32 -> x0, other arithmetic: 54.2 us -> none  [cell_update(): jax.nn.sigmoid(gate_f) * c_prev + jax.nn.sigmoid(gate_i) * jnp.tanh(gate_g)]
    conv_general_dilated x64 -> x0, other arithmetic: 46.2 us -> none  [conv_valid(): lax.conv_general_dilated(operand, kernel, (1, 1), 'VALID', dimension_numb...]
    dynamic_update_slice x32 -> x0, local copies, waits for them, and re-layouts: 38.1 us -> none  [local_run(): lax.scan(time_step, (h_init, c_init), frames_ext)]
    div x64 -> x0, local copies, waits for them, and re-layouts: 37.9 us -> none  [cell_update(): jax.nn.sigmoid(gate_f) * c_prev + jax.nn.sigmoid(gate_i) * jnp.tanh(gate_g)]
    squeeze x64 -> x1, local copies, waits for them, and re-layouts: 31.9 us -> 0.02 us  [pack_weights(): rec = jnp.concatenate([rec[:, 1], rec[:, 0], rec[:, 2]], axis=1)]
  transfers between devices with their start and end apart: 132 -> 0, of which waited for: 1 -> 0; matrix products, arithmetic and copies ran while one was open for 17% -> 0% of each run, Pallas kernels for 0% -> 0%
where the time goes in v1:
time: 295 us; the launch traced here: 294 us
  Pallas kernels  255 us (86%)
  local copies, waits for them, and re-layouts  34.6 us (12%)
  other arithmetic  3.25 us (1%)
    pallas_call x1, Pallas kernels, local_run(): pl.pallas_call(kernel, out_shape=(jax.ShapeDtypeStruct((STEPS, SAMPLES, T...  255 us
    unnamed x10, local copies, waits for them, and re-layouts  27.8 us

profile of v1, /device:TPU:1, one launch (start us, length us, event | category | flops | bytes accessed | tf_op | source)
XLA Modules:
  0.0 293.9 jit_solution(12493241000828972087)
XLA Ops:
  0.6 0.9 slice_bitcast_fusion.4
  1.5 0.1 maximum_multiply_fusion
  1.6 0.1 maximum_bitcast_fusion.1
  1.7 0.9 slice_multiply_fusion.2
  2.6 0.1 pad_maximum_fusion.3
  2.7 1.3 fusion.12
  4.1 0.2 pad_maximum_fusion.2
  4.3 0.1 fusion.5
  4.5 0.0 copy-start.3
  4.5 0.2 pad_maximum_fusion.w_ref
  4.7 0.9 copy-done.3
  5.6 0.0 copy-start.2
  5.6 0.2 copy_convert_fusion
  5.8 1.2 copy-done.2
  7.0 0.0 copy-start.1
  7.0 0.5 maximum_bitcast_fusion.state_ref
  7.5 1.1 copy-done.1
  8.6 1.9 copy.15
  10.5 3.5 %copy.22.frames_ref = bf16[32,2,48,128]{3,2,1,0:T(8,128)(2,1)} copy(bf16[32,2,48,128]{2,0,3,1:T(8,128)(2,1)} %bitcast.28) | data formatting | bytes 1572864 | tf_op jit(solution)/shard_map/reshape | solution.py:328
  14.0 0.0 copy-start
  14.0 1.1 copy-done
  15.1 255.3 %convlstm.1 = (bf16[32,2,32,48,64]{4,3,2,1,0:T(8,128)(2,1)}, f32[2,32,48,64]{3,2,1,0:T(8,128)S(1)}) custom-call(bf16[32,2,48,128]{3,2,1,0:T(8,128)(2,1)S(1)} %copy-done, f32[32,2,48,128]{3,2,1,0:T(8,128)S(1)} %maximum_bitcast_fusion.state_ref, bf16[4,3,256,256]{3,2,1,0:T(8,128)(2,1)S(1)} %pad_maximum_fusion.w_ref, f32[2,128]{1,0:T(2,128)S(1)} %pad_maximum_fusion.4.bias_ref), custom_call_target="tpu_custom_call" | custom-call | tf_op jit(solution)/shard_map/convlstm/pallas_call | solution.py:331
  270.4 22.3 %copy.37 = bf16[32,2,32,48,64]{4,3,2,1,0:T(8,128)(2,1)} copy(bf16[32,2,32,48,64]{4,3,2,1,0:T(8,128)(2,1)} %get-tuple-element.29) | data formatting | bytes 25165824
  292.7 1.1 copy.38
  (5 shorter events, 0.1 us)
Async XLA Ops:
  4.5 1.1 copy-start.3
  5.6 1.4 copy-start.2
  7.0 1.6 copy-start.1
  14.0 1.1 copy-start

commit v2 on v0

v2 whole, which is shorter than its diff:
```python
import jax
import jax.numpy as jnp
from jax import lax
from jax.experimental import pallas as pl
from jax.experimental.pallas import tpu as pltpu
from jax.sharding import PartitionSpec as P

MESH = pl.DeviceIdType.MESH
F32, BF16 = jnp.float32, jnp.bfloat16

STEPS = 32
SAMPLES = 2
TILE_H = 32
TILE_W = 48
C_IN = 4
C_HID = 64
ROUND = 4
ROUNDS = STEPS // ROUND
EXT = 8
WIDE = TILE_W + EXT
PITCH = 64
ROWS = TILE_H + 2 * ROUND
LANES = 128
HALF = LANES // 2
STRIP = ROUND * TILE_W
EDGE = TILE_H // 2 * EXT
EDGE_HALO = ROWS // 2 * EXT
CORNER = ROUND // 2 * EXT
SLOTS = 3 * SAMPLES


def kernel(frames_ref, h_ref, c_ref, w_ref, bias_ref, seq_ref, c_out_ref,
           h_buf, c_buf, g_buf, a_buf, out_buf,
           up_buf, down_buf, edge_buf, from_up, from_down, from_edge,
           send_sem, recv_sem, out_sem):
    row = lax.axis_index("rows")
    col = lax.axis_index("cols")
    has_up = row > 0
    has_down = row < lax.axis_size("rows") - 1
    is_left = col == 0
    other = 1 - col

    own_at = jnp.where(is_left, 0, EXT)
    edge_at = jnp.where(is_left, TILE_W - EXT, EXT)
    halo_at = jnp.where(is_left, TILE_W, 0)
    up_keep = has_up.astype(F32)
    down_keep = has_down.astype(F32)

    def lane_of(cells):
        return lax.broadcasted_iota(jnp.int32, (cells, LANES), 1)

    def low(cells):
        return lane_of(cells) < HALF

    def aligned(at):
        return pl.multiple_of(at, EXT)

    zero = jnp.zeros((WIDE, LANES), F32)
    tail = jnp.zeros((PITCH - WIDE, LANES), F32)

    @pl.loop(0, ROWS)
    def _(y):
        for s in range(SAMPLES):
            at = pl.ds(aligned(y * WIDE), WIDE)
            h_buf[s, at, :] = zero
            c_buf[s, at, :] = zero
            g_buf[s, at, :] = zero
        a_buf[1, pl.ds(pl.multiple_of(y * PITCH, PITCH), PITCH), 0:LANES] = jnp.zeros((PITCH, LANES), BF16)

    for slot in range(SLOTS):
        for at in (0, EDGE_HALO - CORNER):
            from_edge[slot, pl.ds(at, CORNER), :] = jnp.zeros((CORNER, LANES), F32)

    barrier = pltpu.get_barrier_semaphore()

    def greet(target):
        pl.semaphore_signal(barrier, inc=1, device_id=target, device_id_type=MESH)

    greet({"cols": other})

    @pl.when(has_up)
    def _():
        greet({"rows": row - 1})
        greet({"rows": row - 1, "cols": other})

    @pl.when(has_down)
    def _():
        greet({"rows": row + 1})
        greet({"rows": row + 1, "cols": other})

    pl.semaphore_wait(barrier, 1 + 2 * has_up.astype(jnp.int32) + 2 * has_down.astype(jnp.int32))

    def copies(slot):
        def copy(src, dst, index, target):
            return pltpu.make_async_remote_copy(
                src_ref=src, dst_ref=dst, send_sem=send_sem.at[slot, index],
                recv_sem=recv_sem.at[slot, index], device_id=target, device_id_type=MESH)

        edge = edge_buf.at[slot]
        halo = from_edge.at[slot]
        return (
            copy(up_buf.at[slot], from_down.at[slot], 0, {"rows": row - 1}),
            copy(down_buf.at[slot], from_up.at[slot], 1, {"rows": row + 1}),
            copy(edge, halo.at[pl.ds(CORNER, EDGE)], 2, {"cols": other}),
            copy(edge.at[pl.ds(0, CORNER)], halo.at[pl.ds(CORNER + EDGE, CORNER)], 3, {"rows": row - 1, "cols": other}),
            copy(edge.at[pl.ds(EDGE - CORNER, CORNER)], halo.at[pl.ds(0, CORNER)], 4, {"rows": row + 1, "cols": other}),
        )

    cell = lax.broadcasted_iota(jnp.int32, (EXT, LANES), 0)

    def send(slot, read):
        up, down, across, across_up, across_down = copies(slot)

        @pl.loop(0, TILE_H // 2, unroll=8)
        def _(y):
            at = (ROUND + 2 * y) * WIDE + edge_at
            first = read(aligned(at), EXT)
            second = read(aligned(at + WIDE), EXT)
            first = jnp.where(is_left, pltpu.roll(first, EXT // 2, 0), first)
            second = jnp.where(is_left, second, pltpu.roll(second, EXT // 2, 0))
            edge_buf[slot, pl.ds(aligned(y * EXT), EXT), :] = jnp.where(cell < EXT // 2, first, second)

        across.start()
        for r in range(ROUND):
            up_buf[slot, pl.ds(r * TILE_W, TILE_W), :] = read(aligned((ROUND + r) * WIDE + own_at), TILE_W)
            down_buf[slot, pl.ds(r * TILE_W, TILE_W), :] = read(aligned((TILE_H + r) * WIDE + own_at), TILE_W)

        @pl.when(has_up)
        def _():
            up.start()
            across_up.start()

        @pl.when(has_down)
        def _():
            down.start()
            across_down.start()

    def receive(slot, write):
        up, down, across, across_up, across_down = copies(slot)

        @pl.when(has_up)
        def _():
            up.wait_send()
            across_up.wait_send()
            down.wait_recv()
            across_down.wait_recv()
            for r in range(ROUND):
                write(aligned(r * WIDE + own_at), from_up[slot, pl.ds(r * TILE_W, TILE_W), :])

        @pl.when(has_down)
        def _():
            down.wait_send()
            across_down.wait_send()
            up.wait_recv()
            across_up.wait_recv()
            for r in range(ROUND):
                write(aligned((ROUND + TILE_H + r) * WIDE + own_at), from_down[slot, pl.ds(r * TILE_W, TILE_W), :])

        across.wait_send()
        across.wait_recv()

        @pl.loop(0, ROWS // 2, unroll=10)
        def _(y):
            got = from_edge[slot, pl.ds(aligned(y * EXT), EXT), :]
            turned = pltpu.roll(got, EXT // 2, 0)
            at = 2 * y * WIDE + halo_at
            write(aligned(at), jnp.where(is_left, got, turned))
            write(aligned(at + WIDE), jnp.where(is_left, turned, got))

    def frames_io(s):
        def read(at, cells):
            return g_buf[s, pl.ds(at, cells), :]

        def write(at, value):
            g_buf[s, pl.ds(at, value.shape[0]), :] = value

        return read, write

    def state_io(s):
        def read(at, cells):
            return jnp.where(low(cells), h_buf[s, pl.ds(at, cells), :], c_buf[s, pl.ds(at, cells), :])

        def write(at, value):
            cells = value.shape[0]
            h_buf[s, pl.ds(at, cells), :] = value
            c_buf[s, pl.ds(at, cells), :] = jnp.where(low(cells), pltpu.roll(value, HALF, 1), value)

        return read, write

    def frames_slot(s):
        return 2 * SAMPLES + s

    for s in range(SAMPLES):
        @pl.loop(0, TILE_H, unroll=2)
        def _(y):
            at = aligned((ROUND + y) * WIDE + own_at)
            frames_io(s)[1](at, frames_ref[s, y, :, :].astype(F32))

        send(frames_slot(s), frames_io(s)[0])

        @pl.loop(0, TILE_H, unroll=2)
        def _(y):
            at = aligned((ROUND + y) * WIDE + own_at)
            state = jnp.concatenate([h_ref[s, y, :, :].astype(F32), c_ref[s, y, :, :]], axis=1)
            state_io(s)[1](at, state)

        send(2 * s, state_io(s)[0])

    def build(s, n, y):
        at = pl.ds(aligned(y * WIDE), WIDE)
        frames = pltpu.roll(g_buf[s, at, :], lax.rem(HALF + LANES - ROUND * C_IN * n, LANES), 1)
        here = jnp.concatenate([jnp.where(low(WIDE), h_buf[s, at, :], frames), tail])
        before = pltpu.roll(here, 1, 0)
        after = pltpu.roll(here, PITCH - 1, 0)
        lane = lane_of(PITCH)
        first = jnp.where(low(PITCH), here, pltpu.roll(before, HALF, 1))
        second = jnp.where(lane < 80, after, jnp.where(lane < 96, pltpu.roll(here, 16, 1), pltpu.roll(before, 32, 1)))
        second = second.astype(BF16)
        to = pl.ds(pl.multiple_of(y * PITCH, PITCH), PITCH)
        a_buf[0, to, 0:LANES] = first.astype(BF16)
        a_buf[0, to, LANES:2 * LANES] = second
        a_buf[1, to, LANES:2 * LANES] = second

    def advance(s, j, slot):
        step = j - 1
        old, new = step % 2, 1 - step % 2
        count = ROWS - 2 * j
        gates = None
        for dy in range(3):
            left = a_buf[old, pl.ds((j + dy - 1) * PITCH, count * PITCH), :]
            term = jnp.dot(left, w_ref[step, dy, :, :], preferred_element_type=F32)
            gates = term if gates is None else gates + term
        gain = jnp.where(low(1), 0.5, 1.0)
        shift = jnp.where(low(1), 0.5, 0.0)
        for r in range(count):
            y = j + r
            part = slice(r * PITCH, r * PITCH + WIDE)
            here = pl.ds(y * WIDE, WIDE)
            first = jnp.tanh(gates[part, 0:LANES] + bias_ref[0:1, :])
            second = jnp.tanh(gates[part, LANES:] + bias_ref[1:2, :])
            mixed = (0.5 * first + 0.5) * jnp.where(low(WIDE), c_buf[s, here, :], second)
            c_next = mixed + pltpu.roll(mixed, HALF, 1)
            c_buf[s, here, :] = c_next
            h_next = (second * gain + shift) * jnp.tanh(c_next)
            if y < ROUND:
                h_next = h_next * up_keep
            elif y >= ROUND + TILE_H:
                h_next = h_next * down_keep
            else:
                own = jnp.where(is_left, h_next[0:TILE_W, :], h_next[EXT:WIDE, :])
                out_buf[slot, y - ROUND, :, :] = own[:, 0:C_HID].astype(BF16)
            if j == ROUND:
                h_buf[s, here, :] = h_next
            else:
                wide = jnp.concatenate([h_next, tail])
                before = pltpu.roll(wide, 1, 0)
                after = pltpu.roll(wide, PITCH - 1, 0)
                to = pl.ds(y * PITCH, PITCH)
                a_buf[new, to, 0:LANES] = jnp.where(low(PITCH), wide, pltpu.roll(before, HALF, 1)).astype(BF16)
                a_buf[new, to, LANES:LANES + HALF] = after[:, 0:HALF].astype(BF16)

    def out_copy(t, s, slot):
        return pltpu.make_async_copy(out_buf.at[slot], seq_ref.at[t, s], out_sem.at[slot])

    for s in range(SAMPLES):
        receive(frames_slot(s), frames_io(s)[1])

    @pl.loop(0, SAMPLES * ROUNDS)
    def _(turn):
        s = lax.rem(turn, SAMPLES)
        n = lax.div(turn, SAMPLES)
        receive(2 * s + lax.rem(n, 2), state_io(s)[1])

        @pl.loop(0, ROWS, unroll=4)
        def _(y):
            build(s, n, y)

        for j in range(1, ROUND + 1):
            slot = (j - 1) % 2
            if j <= 2:
                pl.when(turn > 0)(lambda: out_copy(0, 0, slot).wait())
            else:
                out_copy(0, 0, slot).wait()
            advance(s, j, slot)
            out_copy(ROUND * n + j - 1, s, slot).start()

        @pl.when(n < ROUNDS - 1)
        def _():
            send(2 * s + lax.rem(n + 1, 2), state_io(s)[0])

    for slot in range(2):
        out_copy(0, 0, slot).wait()

    for s in range(SAMPLES):
        @pl.loop(0, TILE_H, unroll=2)
        def _(y):
            at = aligned((ROUND + y) * WIDE + own_at)
            c_out_ref[s, y, :, :] = c_buf[s, pl.ds(at, TILE_W), 0:C_HID]


def pack_weights(w_in, w_rec):
    def gates(w):
        i, f, o, g = jnp.split(w, 4, axis=-1)
        half = jnp.asarray(0.5, w.dtype)
        return jnp.concatenate([f * half, i * half, o * half, g], axis=-1)

    rec = gates(w_rec)
    rec = jnp.concatenate([rec[:, 1], rec[:, 0], rec[:, 2]], axis=1)
    inp = gates(w_in)[:, ::-1]
    rest = LANES - HALF - 3 * ROUND * C_IN
    packed = []
    for step in range(ROUND):
        spread = jnp.pad(inp, ((0, 0), (0, 0), (step * C_IN, (ROUND - 1 - step) * C_IN), (0, 0)))
        spread = spread.reshape(3, 3 * ROUND * C_IN, 4 * C_HID)
        packed.append(jnp.concatenate([rec, jnp.pad(spread, ((0, 0), (0, rest), (0, 0)))], axis=1))
    return jnp.stack(packed)


def pack_bias(bias):
    i, f, o, g = jnp.split(bias, 4)
    return jnp.stack([jnp.concatenate([f, i]) * 0.5, jnp.concatenate([o * 0.5, g])])


def solution(mesh):
    assert mesh.shape["cols"] == 2
    seq_spec = P(None, "dp", "rows", "cols", None)
    state_spec = P("dp", "rows", "cols", None)

    def local_run(frames, w_in, w_rec, gate_bias, h_init, c_init):
        frames_cells = frames.transpose(1, 2, 3, 0, 4).reshape(SAMPLES, TILE_H, TILE_W, STEPS * C_IN)
        vmem = pl.BlockSpec(memory_space=pltpu.VMEM)
        return pl.pallas_call(
            kernel,
            out_shape=(
                jax.ShapeDtypeStruct((STEPS, SAMPLES, TILE_H, TILE_W, C_HID), BF16),
                jax.ShapeDtypeStruct((SAMPLES, TILE_H, TILE_W, C_HID), F32),
            ),
            in_specs=[vmem] * 5,
            out_specs=(pl.BlockSpec(memory_space=pl.ANY), vmem),
            scratch_shapes=[
                pltpu.VMEM((SAMPLES, ROWS * WIDE, LANES), F32),
                pltpu.VMEM((SAMPLES, ROWS * WIDE, LANES), F32),
                pltpu.VMEM((SAMPLES, ROWS * WIDE, LANES), F32),
                pltpu.VMEM((2, ROWS * PITCH, 2 * LANES), BF16),
                pltpu.VMEM((2, TILE_H, TILE_W, C_HID), BF16),
                pltpu.VMEM((SLOTS, STRIP, LANES), F32),
                pltpu.VMEM((SLOTS, STRIP, LANES), F32),
                pltpu.VMEM((SLOTS, EDGE, LANES), F32),
                pltpu.VMEM((SLOTS, STRIP, LANES), F32),
                pltpu.VMEM((SLOTS, STRIP, LANES), F32),
                pltpu.VMEM((SLOTS, EDGE_HALO, LANES), F32),
                pltpu.SemaphoreType.DMA((SLOTS, 5)),
                pltpu.SemaphoreType.DMA((SLOTS, 5)),
                pltpu.SemaphoreType.DMA((2,)),
            ],
            compiler_params=pltpu.CompilerParams(
                collective_id=0, has_side_effects=True, vmem_limit_bytes=48 * 1024 * 1024),
            name="convlstm",
        )(frames_cells, h_init, c_init, pack_weights(w_in, w_rec), pack_bias(gate_bias))

    return jax.shard_map(
        local_run, mesh=mesh, in_specs=(seq_spec, P(), P(), P(), state_spec, state_spec),
        out_specs=(seq_spec, state_spec), check_vma=False)
```

time: 921 us -> 233 us (0.25)
  starting transfers between devices: 385 us -> 0 us
  Pallas kernels: 0 us -> 197 us
  local copies, waits for them, and re-layouts: 220 us -> 30.9 us
  other arithmetic: 157 us -> 3.75 us
  matrix products: 148 us -> 0 us
    ppermute x132 -> x0, starting transfers between devices: 385 us -> none  [the longest x66 279 us: edge_exchange(): from_prev = lax.ppermute(high_part, axis_name, forward)]
    pallas_call x0 -> x1, Pallas kernels: none -> 197 us  [local_run(): pl.pallas_call(kernel, out_shape=(jax.ShapeDtypeStruct((STEPS, SAMPLES, T...]
    conv_general_dilated x64 -> x0, matrix products: 148 us -> none  [conv_valid(): lax.conv_general_dilated(operand, kernel, (1, 1), 'VALID', dimension_numb...]
    div x32 -> x0, other arithmetic: 54.2 us -> none  [cell_update(): jax.nn.sigmoid(gate_f) * c_prev + jax.nn.sigmoid(gate_i) * jnp.tanh(gate_g)]
    conv_general_dilated x64 -> x0, other arithmetic: 46.2 us -> none  [conv_valid(): lax.conv_general_dilated(operand, kernel, (1, 1), 'VALID', dimension_numb...]
    dynamic_update_slice x32 -> x0, local copies, waits for them, and re-layouts: 38.1 us -> none  [local_run(): lax.scan(time_step, (h_init, c_init), frames_ext)]
    div x64 -> x0, local copies, waits for them, and re-layouts: 37.9 us -> none  [cell_update(): jax.nn.sigmoid(gate_f) * c_prev + jax.nn.sigmoid(gate_i) * jnp.tanh(gate_g)]
    squeeze x64 -> x1, local copies, waits for them, and re-layouts: 31.9 us -> 0.02 us  [pack_weights(): rec = jnp.concatenate([rec[:, 1], rec[:, 0], rec[:, 2]], axis=1)]
  transfers between devices with their start and end apart: 132 -> 0, of which waited for: 1 -> 0; matrix products, arithmetic and copies ran while one was open for 17% -> 0% of each run, Pallas kernels for 0% -> 0%
where the time goes in v2:
time: 233 us; the launch traced here: 232 us
  Pallas kernels  197 us (85%)
  local copies, waits for them, and re-layouts  30.9 us (13%)
  other arithmetic  3.75 us (2%)
    pallas_call x1, Pallas kernels, local_run(): pl.pallas_call(kernel, out_shape=(jax.ShapeDtypeStruct((STEPS, SAMPLES, T...  197 us
    unnamed x8, local copies, waits for them, and re-layouts  24.3 us

profile of v2, /device:TPU:1, one launch (start us, length us, event | category | flops | bytes accessed | tf_op | source)
XLA Modules:
  0.0 232.1 jit_solution(828526848888958819)
XLA Ops:
  0.6 0.9 slice_bitcast_fusion.4
  1.5 0.1 maximum_multiply_fusion
  1.6 0.1 maximum_bitcast_fusion
  1.7 0.9 slice_multiply_fusion.2
  2.6 0.1 pad_maximum_fusion.3
  2.7 1.3 fusion.12
  4.1 0.2 pad_maximum_fusion.2
  4.3 0.1 fusion.5
  4.5 0.0 copy-start.2
  4.5 1.3 pad_maximum_fusion.w_ref
  5.8 0.8 copy-done.2
  6.6 1.9 copy.13
  8.5 0.0 copy-start
  8.5 0.0 copy-start.1
  8.5 3.4 %copy.18.frames_ref = bf16[2,32,48,128]{3,2,1,0:T(8,128)(2,1)S(1)} copy(bf16[2,32,48,128]{2,1,3,0:T(8,128)(2,1)} %bitcast.26) | data formatting | bytes 1572864 | tf_op jit(solution)/shard_map/reshape | solution.py:330
  11.9 0.0 copy-done
  12.0 0.0 copy-done.1
  12.0 196.7 %convlstm.1 = (bf16[32,2,32,48,64]{4,3,2,1,0:T(8,128)(2,1)}, f32[2,32,48,64]{3,2,1,0:T(8,128)S(1)}) custom-call(bf16[2,32,48,128]{3,2,1,0:T(8,128)(2,1)S(1)} %copy.18.frames_ref, bf16[2,32,48,64]{3,2,1,0:T(8,128)(2,1)S(1)} %copy-done.1, f32[2,32,48,64]{3,2,1,0:T(8,128)S(1)} %copy-done, bf16[4,3,256,256]{3,2,1,0:T(8,128)(2,1)} %pad_maximum_fusion.w_ref, ...), custom_call_target="tpu_custom_call" | custom-call | tf_op jit(solution)/shard_map/convlstm/pallas_call | solution.py:332
  208.7 22.3 %copy.30 = bf16[32,2,32,48,64]{4,3,2,1,0:T(8,128)(2,1)} copy(bf16[32,2,32,48,64]{4,3,2,1,0:T(8,128)(2,1)} %get-tuple-element.29) | data formatting | bytes 25165824
  231.0 1.1 copy.31
  (6 shorter events, 0.1 us)
Async XLA Ops:
  4.5 2.2 copy-start.2
  8.5 3.4 %copy-start = (f32[2,32,48,64]{3,2,1,0:T(8,128)S(1)}, f32[2,32,48,64]{3,2,1,0:T(8,128)}, u32[]{:S(2)}) copy-start(f32[2,32,48,64]{3,2,1,0:T(8,128)} %c_ref.1) | copy-start | bytes 2359300
  8.5 3.4 %copy-start.1 = (bf16[2,32,48,64]{3,2,1,0:T(8,128)(2,1)S(1)}, bf16[2,32,48,64]{3,2,1,0:T(8,128)(2,1)}, u32[]{:S(2)}) copy-start(bf16[2,32,48,64]{3,2,1,0:T(8,128)(2,1)} %h_ref.1) | copy-start | bytes 1179652

commit v3 on v2

--- a/solution.py
+++ b/solution.py
@@ -18,7 +18,9 @@
 ROUNDS = STEPS // ROUND
 EXT = 8
 WIDE = TILE_W + EXT
+PHASES = WIDE // 8
 PITCH = 64
+SUB_ROWS = 8
 ROWS = TILE_H + 2 * ROUND
 LANES = 128
 HALF = LANES // 2
@@ -30,9 +32,9 @@
 
 
 def kernel(frames_ref, h_ref, c_ref, w_ref, bias_ref, seq_ref, c_out_ref,
-           h_buf, c_buf, g_buf, a_buf, out_buf,
+           s_buf, c_buf, g_buf, a_buf,
            up_buf, down_buf, edge_buf, from_up, from_down, from_edge,
-           send_sem, recv_sem, out_sem):
+           send_sem, recv_sem):
     row = lax.axis_index("rows")
     col = lax.axis_index("cols")
     has_up = row > 0
@@ -62,10 +64,8 @@
     def _(y):
         for s in range(SAMPLES):
             at = pl.ds(aligned(y * WIDE), WIDE)
-            h_buf[s, at, :] = zero
-            c_buf[s, at, :] = zero
+            s_buf[s, at, :] = zero
             g_buf[s, at, :] = zero
-        a_buf[1, pl.ds(pl.multiple_of(y * PITCH, PITCH), PITCH), 0:LANES] = jnp.zeros((PITCH, LANES), BF16)
 
     for slot in range(SLOTS):
         for at in (0, EDGE_HALO - CORNER):
@@ -167,25 +167,20 @@
             write(aligned(at), jnp.where(is_left, got, turned))
             write(aligned(at + WIDE), jnp.where(is_left, turned, got))
 
+    def cells_of(buf, s):
+        def read(at, cells):
+            return buf[s, pl.ds(at, cells), :]
+
+        def write(at, value):
+            buf[s, pl.ds(at, value.shape[0]), :] = value
+
+        return read, write
+
     def frames_io(s):
-        def read(at, cells):
-            return g_buf[s, pl.ds(at, cells), :]
-
-        def write(at, value):
-            g_buf[s, pl.ds(at, value.shape[0]), :] = value
-
-        return read, write
+        return cells_of(g_buf, s)
 
     def state_io(s):
-        def read(at, cells):
-            return jnp.where(low(cells), h_buf[s, pl.ds(at, cells), :], c_buf[s, pl.ds(at, cells), :])
-
-        def write(at, value):
-            cells = value.shape[0]
-            h_buf[s, pl.ds(at, cells), :] = value
-            c_buf[s, pl.ds(at, cells), :] = jnp.where(low(cells), pltpu.roll(value, HALF, 1), value)
-
-        return read, write
+        return cells_of(s_buf, s)
 
     def frames_slot(s):
         return 2 * SAMPLES + s
@@ -206,61 +201,75 @@
 
         send(2 * s, state_io(s)[0])
 
+    def interleaved(buf, s, y):
+        return jnp.concatenate([buf[s, pl.ds(y * WIDE + v, 8, PHASES), :] for v in range(PHASES)])
+
+    def before(value):
+        first = jnp.where(cell == 0, 0.0, pltpu.roll(value[WIDE - 8:WIDE, :], 1, 0))
+        return jnp.concatenate([first, value[0:WIDE - 8, :]])
+
+    def after(value):
+        last = jnp.where(cell == 7, 0.0, pltpu.roll(value[0:8, :], 7, 0))
+        return jnp.concatenate([value[8:WIDE, :], last])
+
+    def operand(value):
+        return jnp.concatenate([value, tail]).astype(BF16)
+
     def build(s, n, y):
-        at = pl.ds(aligned(y * WIDE), WIDE)
-        frames = pltpu.roll(g_buf[s, at, :], lax.rem(HALF + LANES - ROUND * C_IN * n, LANES), 1)
-        here = jnp.concatenate([jnp.where(low(WIDE), h_buf[s, at, :], frames), tail])
-        before = pltpu.roll(here, 1, 0)
-        after = pltpu.roll(here, PITCH - 1, 0)
-        lane = lane_of(PITCH)
-        first = jnp.where(low(PITCH), here, pltpu.roll(before, HALF, 1))
-        second = jnp.where(lane < 80, after, jnp.where(lane < 96, pltpu.roll(here, 16, 1), pltpu.roll(before, 32, 1)))
-        second = second.astype(BF16)
+        state = interleaved(s_buf, s, y)
+        turned = pltpu.roll(state, HALF, 1)
+        c_buf[s, pl.ds(aligned(y * WIDE), WIDE), :] = turned
+        frames = interleaved(g_buf, s, y)
+
+        def frames_to(lane):
+            return pltpu.roll(frames, lax.rem(lane + LANES - ROUND * C_IN * n, LANES), 1)
+
+        lane = lane_of(WIDE)
+        right = after(jnp.where(low(WIDE), state, frames_to(64)))
+        second = jnp.where(lane < 80, right, jnp.where(lane < 96, frames_to(80), before(frames_to(96))))
+        second = operand(second)
         to = pl.ds(pl.multiple_of(y * PITCH, PITCH), PITCH)
-        a_buf[0, to, 0:LANES] = first.astype(BF16)
+        a_buf[0, to, 0:LANES] = operand(jnp.where(low(WIDE), state, before(turned)))
         a_buf[0, to, LANES:2 * LANES] = second
         a_buf[1, to, LANES:2 * LANES] = second
 
-    def advance(s, j, slot):
+    def advance(s, t, j):
         step = j - 1
         old, new = step % 2, 1 - step % 2
-        count = ROWS - 2 * j
-        gates = None
-        for dy in range(3):
-            left = a_buf[old, pl.ds((j + dy - 1) * PITCH, count * PITCH), :]
-            term = jnp.dot(left, w_ref[step, dy, :, :], preferred_element_type=F32)
-            gates = term if gates is None else gates + term
         gain = jnp.where(low(1), 0.5, 1.0)
         shift = jnp.where(low(1), 0.5, 0.0)
-        for r in range(count):
-            y = j + r
-            part = slice(r * PITCH, r * PITCH + WIDE)
-            here = pl.ds(y * WIDE, WIDE)
-            first = jnp.tanh(gates[part, 0:LANES] + bias_ref[0:1, :])
-            second = jnp.tanh(gates[part, LANES:] + bias_ref[1:2, :])
-            mixed = (0.5 * first + 0.5) * jnp.where(low(WIDE), c_buf[s, here, :], second)
-            c_next = mixed + pltpu.roll(mixed, HALF, 1)
-            c_buf[s, here, :] = c_next
-            h_next = (second * gain + shift) * jnp.tanh(c_next)
-            if y < ROUND:
-                h_next = h_next * up_keep
-            elif y >= ROUND + TILE_H:
-                h_next = h_next * down_keep
-            else:
-                own = jnp.where(is_left, h_next[0:TILE_W, :], h_next[EXT:WIDE, :])
-                out_buf[slot, y - ROUND, :, :] = own[:, 0:C_HID].astype(BF16)
-            if j == ROUND:
-                h_buf[s, here, :] = h_next
-            else:
-                wide = jnp.concatenate([h_next, tail])
-                before = pltpu.roll(wide, 1, 0)
-                after = pltpu.roll(wide, PITCH - 1, 0)
-                to = pl.ds(y * PITCH, PITCH)
-                a_buf[new, to, 0:LANES] = jnp.where(low(PITCH), wide, pltpu.roll(before, HALF, 1)).astype(BF16)
-                a_buf[new, to, LANES:LANES + HALF] = after[:, 0:HALF].astype(BF16)
-
-    def out_copy(t, s, slot):
-        return pltpu.make_async_copy(out_buf.at[slot], seq_ref.at[t, s], out_sem.at[slot])
+        for top in range(j, ROWS - j, SUB_ROWS):
+            count = min(SUB_ROWS, ROWS - j - top)
+            gates = None
+            for dy in range(3):
+                left = a_buf[old, pl.ds((top + dy - 1) * PITCH, count * PITCH), :]
+                term = jnp.dot(left, w_ref[step, dy, :, :], preferred_element_type=F32)
+                gates = term if gates is None else gates + term
+            for r in range(count):
+                y = top + r
+                part = slice(r * PITCH, r * PITCH + WIDE)
+                here = pl.ds(y * WIDE, WIDE)
+                first = jnp.tanh(gates[part, 0:LANES] + bias_ref[0:1, :])
+                second = jnp.tanh(gates[part, LANES:] + bias_ref[1:2, :])
+                mixed = (0.5 * first + 0.5) * jnp.where(low(WIDE), c_buf[s, here, :], second)
+                c_next = mixed + pltpu.roll(mixed, HALF, 1)
+                h_next = (second * gain + shift) * jnp.tanh(c_next)
+                if y < ROUND:
+                    h_next = h_next * up_keep
+                elif y >= ROUND + TILE_H:
+                    h_next = h_next * down_keep
+                else:
+                    state = h_next if j < ROUND else jnp.where(low(WIDE), h_next, c_next)
+                    for v in range(PHASES):
+                        s_buf[s, pl.ds(y * WIDE + v, 8, PHASES), :] = state[8 * v:8 * v + 8, :]
+                    own = s_buf[s, pl.ds(aligned(y * WIDE + own_at), TILE_W), :]
+                    seq_ref[t, s, y - ROUND, :, :] = own[:, 0:C_HID].astype(BF16)
+                if j < ROUND:
+                    c_buf[s, here, :] = c_next
+                    to = pl.ds(y * PITCH, PITCH)
+                    side = jnp.where(low(WIDE), h_next, before(pltpu.roll(h_next, HALF, 1)))
+                    a_buf[new, to, 0:LANES] = operand(side)
+                    a_buf[new, to, LANES:LANES + HALF] = operand(after(h_next))[:, 0:HALF]
 
     for s in range(SAMPLES):
         receive(frames_slot(s), frames_io(s)[1])
@@ -276,26 +285,17 @@
             build(s, n, y)
 
         for j in range(1, ROUND + 1):
-            slot = (j - 1) % 2
-            if j <= 2:
-                pl.when(turn > 0)(lambda: out_copy(0, 0, slot).wait())
-            else:
-                out_copy(0, 0, slot).wait()
-            advance(s, j, slot)
-            out_copy(ROUND * n + j - 1, s, slot).start()
+            advance(s, ROUND * n + j - 1, j)
 
         @pl.when(n < ROUNDS - 1)
         def _():
             send(2 * s + lax.rem(n + 1, 2), state_io(s)[0])
-
-    for slot in range(2):
-        out_copy(0, 0, slot).wait()
 
     for s in range(SAMPLES):
         @pl.loop(0, TILE_H, unroll=2)
         def _(y):
             at = aligned((ROUND + y) * WIDE + own_at)
-            c_out_ref[s, y, :, :] = c_buf[s, pl.ds(at, TILE_W), 0:C_HID]
+            c_out_ref[s, y, :, :] = s_buf[s, pl.ds(at, TILE_W), :][:, HALF:]
 
 
 def pack_weights(w_in, w_rec):
@@ -332,17 +332,16 @@
         return pl.pallas_call(
             kernel,
             out_shape=(
-                jax.ShapeDtypeStruct((STEPS, SAMPLES, TILE_H, TILE_W, C_HID), BF16),
+                pltpu.VMEM((STEPS, SAMPLES, TILE_H, TILE_W, C_HID), BF16),
                 jax.ShapeDtypeStruct((SAMPLES, TILE_H, TILE_W, C_HID), F32),
             ),
             in_specs=[vmem] * 5,
-            out_specs=(pl.BlockSpec(memory_space=pl.ANY), vmem),
+            out_specs=(vmem, vmem),
             scratch_shapes=[
                 pltpu.VMEM((SAMPLES, ROWS * WIDE, LANES), F32),
                 pltpu.VMEM((SAMPLES, ROWS * WIDE, LANES), F32),
                 pltpu.VMEM((SAMPLES, ROWS * WIDE, LANES), F32),
                 pltpu.VMEM((2, ROWS * PITCH, 2 * LANES), BF16),
-                pltpu.VMEM((2, TILE_H, TILE_W, C_HID), BF16),
                 pltpu.VMEM((SLOTS, STRIP, LANES), F32),
                 pltpu.VMEM((SLOTS, STRIP, LANES), F32),
                 pltpu.VMEM((SLOTS, EDGE, LANES), F32),
@@ -351,10 +350,9 @@
                 pltpu.VMEM((SLOTS, EDGE_HALO, LANES), F32),
                 pltpu.SemaphoreType.DMA((SLOTS, 5)),
                 pltpu.SemaphoreType.DMA((SLOTS, 5)),
-                pltpu.SemaphoreType.DMA((2,)),
             ],
             compiler_params=pltpu.CompilerParams(
-                collective_id=0, has_side_effects=True, vmem_limit_bytes=48 * 1024 * 1024),
+                collective_id=0, has_side_effects=True, vmem_limit_bytes=32 * 1024 * 1024),
             name="convlstm",
         )(frames_cells, h_init, c_init, pack_weights(w_in, w_rec), pack_bias(gate_bias))
 

time: 233 us -> 140 us (0.60)
  Pallas kernels: 197 us -> 119 us
  local copies, waits for them, and re-layouts: 30.9 us -> 15.7 us
    pallas_call x1, Pallas kernels: 197 us -> 119 us  [local_run(): pl.pallas_call(kernel, out_shape=(pltpu.VMEM((STEPS, SAMPLES, TILE_H, TIL...]
    unnamed x8 -> x6, local copies, waits for them, and re-layouts: 24.3 us -> 10.9 us
where the time goes in v3:
time: 140 us; the launch traced here: 139 us
  Pallas kernels  119 us (85%)
  local copies, waits for them, and re-layouts  15.7 us (11%)
  other arithmetic  4.34 us (3%)
    pallas_call x1, Pallas kernels, local_run(): pl.pallas_call(kernel, out_shape=(pltpu.VMEM((STEPS, SAMPLES, TILE_H, TIL...  119 us
    unnamed x6, local copies, waits for them, and re-layouts  10.9 us
    reshape x1, local copies, waits for them, and re-layouts, local_run(): frames.transpose(1, 2, 3, 0, 4)  2.88 us

profile of v3, /device:TPU:1, one launch (start us, length us, event | category | flops | bytes accessed | tf_op | source)
XLA Modules:
  0.0 139.3 jit_solution(5837845734823078021)
XLA Ops:
  0.6 0.9 slice_bitcast_fusion.4
  1.5 0.1 maximum_multiply_fusion
  1.6 0.1 maximum_bitcast_fusion
  1.7 0.6 pad_maximum_fusion.4.bias_ref
  2.3 0.9 slice_multiply_fusion.2
  3.1 0.1 pad_maximum_fusion.3
  3.3 1.3 fusion.12
  4.7 0.2 pad_maximum_fusion.2
  4.9 0.1 fusion.5
  5.0 0.0 copy-start
  5.1 1.3 pad_maximum_fusion.w_ref
  6.4 0.8 copy-done
  7.2 0.5 copy.13
  7.8 2.9 %copy.18.frames_ref = bf16[2,32,48,128]{3,2,1,0:T(8,128)(2,1)} copy(bf16[2,32,48,128]{2,1,3,0:T(8,128)(2,1)S(1)} %bitcast.26) | data formatting | bytes 1572864 | tf_op jit(solution)/shard_map/reshape | solution.py:330
  10.6 118.6 %convlstm.1 = (bf16[32,2,32,48,64]{4,3,2,1,0:T(8,128)(2,1)S(1)}, f32[2,32,48,64]{3,2,1,0:T(8,128)}) custom-call(bf16[2,32,48,128]{3,2,1,0:T(8,128)(2,1)} %copy.18.frames_ref, bf16[2,32,48,64]{3,2,1,0:T(8,128)(2,1)} %h_ref.1, f32[2,32,48,64]{3,2,1,0:T(8,128)} %c_ref.1, bf16[4,3,256,256]{3,2,1,0:T(8,128)(2,1)} %pad_maximum_fusion.w_ref, ...), custom_call_target="tpu_custom_call" | custom-call | tf_op jit(solution)/shard_map/convlstm/pallas_call | solution.py:332
  129.2 0.0 copy-start.1
  129.2 8.9 %copy.30 = bf16[32,2,32,48,64]{4,3,2,1,0:T(8,128)(2,1)} copy(bf16[32,2,32,48,64]{4,3,2,1,0:T(8,128)(2,1)S(1)} %get-tuple-element.27) | data formatting | bytes 25165824
  138.1 0.0 copy-done.1
  138.1 1.1 copy.31
  (5 shorter events, 0.1 us)
Async XLA Ops:
  5.0 2.2 %copy-start = (bf16[32,2,32,48,4]{3,4,2,1,0:T(4,128)(2,1)S(1)}, bf16[32,2,32,48,4]{3,4,2,1,0:T(4,128)(2,1)}, u32[]{:S(2)}) copy-start(bf16[32,2,32,48,4]{3,4,2,1,0:T(4,128)(2,1)} %param.6) | copy-start | bytes 2359300
  129.2 8.9 %copy-start.1 = (f32[2,32,48,64]{3,2,1,0:T(8,128)S(1)}, f32[2,32,48,64]{3,2,1,0:T(8,128)}, u32[]{:S(2)}) copy-start(f32[2,32,48,64]{3,2,1,0:T(8,128)} %get-tuple-element.32) | copy-start | bytes 2359300
